TPU v7x, 32 devices: a whole 2x2x4 slice. The times are simulated.
32 devices in a mesh: section: 4 (over y, x), tp: 8 (over z, core).
Axes of the slice: x: 2, y: 2, z: 4, core: 2. Of those that a mesh axis runs over, the one named last changes fastest.
Arguments:
- awaiting_arrivals: bfloat16 [4, 8, 25, 1920], P('section', 'tp'), may hold values from -6 to 6
- label_numbers: int32 [5, 8], replicated, may hold values from 0 to 1000
- drawn_coarse_codes: int32 [1, 8, 30], replicated, may hold values from 0 to 4095
- discrete_prototypes: float32 [4096, 32], replicated, may hold values from -6 to 6
- code_raising_operator: bfloat16 [32, 1920], replicated, may hold values from -1 to 1
- placement_tier_features: bfloat16 [25, 1920], replicated, may hold values from -3 to 3
- label_feature_rows: bfloat16 [1001, 1920], P(None, 'tp'), may hold values from -6 to 6
- conditioned_gain_mapping: bfloat16 [4, 1920, 3, 1920], P('section', None, None, 'tp'), may hold values from -0.125 to 0.125
- conditioned_shift_addend: float32 [4, 3, 1920], P('section', None, 'tp'), may hold values from -3 to 3
- question_answer_operator: bfloat16 [4, 1920, 3, 1920], P('section', None, None, 'tp'), may hold values from -0.125 to 0.125
- mixing_return_operator: bfloat16 [4, 1920, 1920], P('section', None, 'tp'), may hold values from -0.125 to 0.125
- focus_sharpness_exponents: float32 [4, 30], P('section'), may hold values from 1 to 5.5
- prior_resolution_probes: bfloat16 [4, 2, 8, 30, 1920], P('section', None, 'tp'), may hold values from -0.75 to 0.75
- prior_resolution_answers: bfloat16 [4, 2, 8, 30, 1920], P('section', None, 'tp'), may hold values from -6 to 6
Outputs:
- section_out: bfloat16 [4, 2, 8, 25, 1920], P('section', None, 'tp')
Inputs may be any that keep to these rules, and one draw needn't show every extreme that they name: `drawn_coarse_codes`: codebook indices of the maps of sides 1 to 4 of each image, one map after another, each row by row. `label_numbers`: class of each image; row r belongs to the micro-batch r - 4.
All inputs are finite; a program needn't handle non-finite values.
Results may differ from a plain program's by a relative error of at most 0.0151.
Values may be sent and summed in bfloat16 or wider, within the bound.
No kernel may reach another device: no remote copies, remote signals or barrier semaphores. Data moves between devices by JAX's collectives and lax.ppermute only.
A program may use at most 128 MiB of HBM per device.

v0:
```python
import jax
import jax.numpy as jnp
from jax import lax
from jax.sharding import PartitionSpec as P

FOCUS_GROUPS = 30
HEAD_DIM = 64
SIDE = 5
LOG_CAP = 4.605170185988092


def shifted(value, axis, steps):
    count = lax.axis_size(axis)
    first, last = (max(0, -steps), min(count, count - steps))
    return lax.ppermute(value, axis, [(source, source + steps) for source in range(first, last)])


def crossing_matrix(target, coarse):
    fine_index = jnp.arange(target, dtype=jnp.float32)
    coarse_index = jnp.arange(coarse, dtype=jnp.float32)
    begins = jnp.maximum(fine_index[:, None] / target, coarse_index[None, :] / coarse)
    finish = jnp.minimum(
        (fine_index[:, None] + 1.0) / target, (coarse_index[None, :] + 1.0) / coarse
    )
    return jnp.maximum(finish - begins, 0.0) * target


def resampler():
    blocks = []
    for coarse in range(1, SIDE):
        crossing = crossing_matrix(SIDE, coarse)
        blocks.append(
            (crossing[:, None, :, None] * crossing[None, :, None, :]).reshape(
                SIDE * SIDE, coarse * coarse
            )
        )
    return jnp.concatenate(blocks, axis=1)


def embed(
    drawn_coarse_codes,
    discrete_prototypes,
    code_raising_operator,
    placement_tier_features,
    resample_table,
):
    looked_up = discrete_prototypes[drawn_coarse_codes]
    mapped = jnp.einsum(
        "tc,nicv->nitv", resample_table, looked_up, precision=lax.Precision.HIGHEST
    ).astype(jnp.bfloat16)
    leading = mapped.shape[:3]
    projected_rows = jnp.dot(
        mapped.reshape(-1, mapped.shape[3]),
        code_raising_operator,
        preferred_element_type=jnp.float32,
    )
    projected_rows = projected_rows.reshape(leading + (code_raising_operator.shape[1],))
    return (projected_rows + placement_tier_features.astype(jnp.float32)).astype(jnp.bfloat16)


def norm_mod(latent_stream, scale_term, offset_term):
    widened = latent_stream.astype(jnp.float32)
    average = jnp.mean(widened, axis=-1, keepdims=True)
    centred = widened - average
    spread = jnp.mean(centred * centred, axis=-1, keepdims=True)
    normed = (
        centred * lax.rsqrt(spread + 1e-06) * (1.0 + scale_term[:, None, :])
        + offset_term[:, None, :]
    )
    return normed.astype(jnp.bfloat16)


def attention(qkv_cols, log_scale, cached_keys, cached_values):
    qkv = lax.all_to_all(qkv_cols, "tp", split_axis=0, concat_axis=3, tiled=True)
    images = qkv.shape[0]
    count = qkv.shape[1]
    widened = qkv.astype(jnp.float32)
    query = widened[:, :, 0].reshape(images, count, FOCUS_GROUPS, HEAD_DIM)
    new_keys = widened[:, :, 1].reshape(images, count, FOCUS_GROUPS, HEAD_DIM)
    new_values = qkv[:, :, 2].reshape(images, count, FOCUS_GROUPS, HEAD_DIM)
    head_mult = jnp.exp(jnp.minimum(log_scale, LOG_CAP))
    query = (
        query
        * lax.rsqrt(jnp.sum(query * query, axis=-1, keepdims=True) + 1e-06)
        * head_mult[:, None]
    )
    new_keys = new_keys * lax.rsqrt(jnp.sum(new_keys * new_keys, axis=-1, keepdims=True) + 1e-06)
    all_keys = jnp.concatenate(
        [cached_keys.astype(jnp.float32).reshape(images, -1, FOCUS_GROUPS, HEAD_DIM), new_keys],
        axis=1,
    )
    all_values = jnp.concatenate(
        [cached_values.reshape(images, -1, FOCUS_GROUPS, HEAD_DIM), new_values], axis=1
    )
    scores = jnp.einsum("iqhd,ikhd->ihqk", query, all_keys, precision=lax.Precision.HIGHEST)
    maximum = jnp.max(scores, axis=-1, keepdims=True)
    weights = jnp.exp(scores - maximum)
    probabilities = (weights / jnp.sum(weights, axis=-1, keepdims=True)).astype(jnp.bfloat16)
    mixed = jnp.einsum(
        "ihqk,ikhd->iqhd", probabilities, all_values, preferred_element_type=jnp.float32
    )
    return mixed.reshape(images, count, FOCUS_GROUPS * HEAD_DIM).astype(jnp.bfloat16)


def project_out(attended, out_matrix):
    return jnp.dot(
        lax.all_gather(attended, "tp", axis=0, tiled=True),
        out_matrix,
        preferred_element_type=jnp.float32,
    )


def pass_on(latent_stream):
    return shifted(latent_stream, "section", 1)


def local(
    awaiting_arrivals,
    label_numbers,
    drawn_coarse_codes,
    discrete_prototypes,
    code_raising_operator,
    placement_tier_features,
    label_feature_rows,
    conditioned_gain_mapping,
    conditioned_shift_addend,
    question_answer_operator,
    mixing_return_operator,
    focus_sharpness_exponents,
    prior_resolution_probes,
    prior_resolution_answers,
):
    sections = lax.axis_size("section")
    section_at = lax.axis_index("section")
    group_index = lax.axis_index("tp")
    moments = prior_resolution_probes.shape[1]
    width = question_answer_operator.shape[1]
    column_width = question_answer_operator.shape[3]
    images = drawn_coarse_codes.shape[1]
    resident_pictures = awaiting_arrivals.shape[1]
    class_rows = lax.dynamic_slice_in_dim(label_numbers, sections - 1 - section_at, moments, 0)
    class_part = jnp.take(label_feature_rows, class_rows, axis=0)
    activated_part = jax.nn.silu(class_part.astype(jnp.float32)).astype(jnp.bfloat16)
    gated_response = lax.all_gather(activated_part, "tp", axis=2, tiled=True)
    flat_active = gated_response.reshape(moments * images, width)
    inner_block = 0
    local_mod = conditioned_gain_mapping[inner_block].reshape(width, 3 * column_width)
    modulated = jnp.dot(flat_active, local_mod, preferred_element_type=jnp.float32)
    mod_list = [
        modulated.reshape(moments, images, 3, column_width) + conditioned_shift_addend[inner_block]
    ]
    mod_cols = jnp.stack(mod_list)
    resample_table = resampler()
    emitted = []
    mod_rows = lax.all_to_all(mod_cols, "tp", split_axis=2, concat_axis=4, tiled=True)
    own_tokens = lax.dynamic_slice_in_dim(
        drawn_coarse_codes, group_index * resident_pictures, resident_pictures, 1
    )
    entering = embed(
        own_tokens,
        discrete_prototypes,
        code_raising_operator,
        placement_tier_features,
        resample_table,
    )
    passed_along_activation = awaiting_arrivals[0]
    for clock_tick in range(moments):
        latent_stream = passed_along_activation
        inner_block = 0
        modulation = mod_rows[inner_block, clock_tick]
        normed = norm_mod(latent_stream, modulation[:, 1], modulation[:, 2])
        local_qkv = question_answer_operator[inner_block].reshape(width, 3 * column_width)

        def body_product(portion, offset, local_qkv=local_qkv):
            return jnp.dot(portion, local_qkv, preferred_element_type=jnp.float32).astype(
                jnp.bfloat16
            )

        qkv_cols = body_product(lax.all_gather(normed, "tp", axis=0, tiled=True), jnp.int32(0))
        qkv_cols = qkv_cols.reshape(qkv_cols.shape[0], qkv_cols.shape[1], 3, column_width)
        attended = attention(
            qkv_cols,
            focus_sharpness_exponents[inner_block],
            prior_resolution_probes[inner_block, clock_tick],
            prior_resolution_answers[inner_block, clock_tick],
        )
        projected_cols = project_out(attended, mixing_return_operator[inner_block]).astype(
            jnp.bfloat16
        )
        projected = lax.all_to_all(projected_cols, "tp", split_axis=0, concat_axis=2, tiled=True)
        latent_stream = (
            latent_stream.astype(jnp.float32)
            + modulation[:, 0][:, None, :] * projected.astype(jnp.float32)
        ).astype(jnp.bfloat16)
        emitted.append(latent_stream)
        if clock_tick + 1 < moments:
            arrived = pass_on(latent_stream)
            passed_along_activation = jnp.where(section_at == 0, entering[clock_tick], arrived)
    result = jnp.stack(emitted)
    return result[None]


def solution(mesh):
    in_specs = (
        P("section", "tp", None, None),
        P(),
        P(),
        P(),
        P(),
        P(),
        P(None, "tp"),
        P("section", None, None, "tp"),
        P("section", None, "tp"),
        P("section", None, None, "tp"),
        P("section", None, "tp"),
        P("section", None),
        P("section", None, "tp", None, None),
        P("section", None, "tp", None, None),
    )
    out_specs = P("section", None, "tp", None, None)
    return jax.shard_map(local, mesh=mesh, in_specs=in_specs, out_specs=out_specs, check_vma=False)
```

profile of v0, /device:TPU:4, one launch (start us, length us, event | category | flops | bytes accessed | tf_op | source)
XLA Modules:
  0.0 244.2 jit_solution(13599707762112273153)
XLA Ops:
  0.9 1.2 copy.162
  3.0 16.4 %all_gather.15 = bf16[2,8,1920]{1,0,2:T(2,128)(2,1)S(1)} all-gather(bf16[2,8,240]{1,0,2:T(2,128)(2,1)S(1)} %copy.163), channel_id=1, replica_groups=mesh['section'=4,'tp'=8] {'tp'}, dimensions={2}, use_global_device_ids=true | all-gather | bytes 69120 | tf_op jit(solution)/shard_map/all_gather | solution.py:144
  20.1 2.9 %fusion.17 = f32[1,2,8,3,240]{4,2,3,1,0:T(8,128)S(1)} fusion(bf16[1,1920,3,240]{1,3,2,0:T(8,128)(2,1)} %param.21, bf16[2,8,1920,1]{1,0,2,3:T(2,128)(2,1)S(1)} %bitcast.178, f32[3,240]{1,0:T(4,128)S(1)} %bitcast.180), kind=kOutput, calls=%fused_computation.24 | convolution fusion | flops 44248320 | bytes 2875200 | tf_op jit(solution)/shard_map/dot_general | solution.py:148
  23.7 5.1 %all-to-all-start = ((f32[1,2,8,3,240]{4,1,3,0,2:T(2,128)}), f32[1,2,8,3,240]{4,1,3,0,2:T(2,128)S(1)}, u32[]{:S(2)}, u32[]{:S(2)}) async-start(f32[1,2,8,3,240]{4,1,3,0,2:T(2,128)} %copy.165), calls=%async_computation | async-start | bytes 98304 | tf_op jit(solution)/shard_map/all_to_all | solution.py:155
  29.2 1.5 convert_reduce_fusion.1
  32.4 2.8 %slice_reduce_fusion = (bf16[30,1920]{1,0:T(8,128)(2,1)}, bf16[30,1920]{1,0:T(8,128)(2,1)}) fusion(bf16[1,2,1,30,1920]{4,1,3,2,0:T(2,128)(2,1)} %param.27), kind=kLoop, calls=%fused_computation.77 | loop fusion | bytes 460800 | tf_op jit(solution)/shard_map/slice | solution.py:185
  36.7 17.0 %all_gather.16 = bf16[8,25,1920]{2,1,0:T(8,128)(2,1)S(1)} all-gather(bf16[1,25,1920]{2,1,0:T(8,128)(2,1)S(1)} %fusion.43), channel_id=1, replica_groups=mesh['section'=4,'tp'=8] {'tp'}, dimensions={0}, use_global_device_ids=true | all-gather | bytes 864000 | tf_op jit(solution)/shard_map/all_gather | solution.py:179
  53.6 1.8 convolution_convert_fusion.1
  55.4 1.7 reshape.1148
  58.0 5.2 %all-to-all-start.1 = ((bf16[8,25,3,240]{3,1,2,0:T(8,128)(2,1)}), bf16[8,25,3,240]{3,1,2,0:T(8,128)(2,1)}, u32[]{:S(2)}, u32[]{:S(2)}) async-start(bf16[8,25,3,240]{3,1,2,0:T(8,128)(2,1)} %copy.169), calls=%async_computation.1 | async-start | bytes 786432 | tf_op jit(solution)/shard_map/all_to_all | solution.py:74
  67.0 3.0 %copy.180 = f32[4096,32]{1,0:T(8,128)} copy(f32[4096,32]{0,1:T(8,128)} %param.17) | data formatting | bytes 1048576 | tf_op args[3]
  73.9 2.8 %gather_fusion.1 = f32[30,32]{1,0:T(8,128)} fusion(f32[4096,32]{1,0:T(8,128)} %copy.180, s32[1024]{0:T(1024)S(1)} %pad_clamp_fusion), kind=kCustom, calls=%fused_computation.1 | custom fusion | bytes 7800 | tf_op jit(solution)/shard_map/gather | solution.py:47
  82.2 1.4 copy.173
  83.6 1.8 copy_multiply_fusion.1
  86.5 1.7 slice_multiply_fusion.1
  88.1 1.9 mul.390
  91.4 2.8 %fusion.24 = f32[30,25,55]{2,1,0:T(8,128)S(1)} fusion(f32[1,25,30,64]{3,1,2,0:T(8,128)} %copy_multiply_fusion.1, f32[1,30,30,64]{3,1,2,0:T(8,128)} %copy.175, f32[25,30,64]{2,1,0:T(8,128)S(1)} %multiply_multiply_fusion.1), kind=kOutput, calls=%fused_computation.31 | convolution fusion | flops 31785600 | bytes 779400 | tf_op jit(solution)/shard_map/iqhd,ikhd->ihqk/dot_general | solution.py:95
  95.5 1.7 copy.172
  97.2 3.5 %fusion.12 = bf16[1,25,30,64]{3,1,2,0:T(8,128)(2,1)} fusion(bf16[1,25,30,64]{3,1,2,0:T(8,128)(2,1)} %copy.172, bf16[1,30,30,64]{3,1,2,0:T(8,128)(2,1)} %copy.171, f32[30,25]{1,0:T(8,128)S(1)} %fusion.73, f32[30,25,55]{2,1,0:T(8,128)S(1)} %fusion.24), kind=kOutput, calls=%fused_computation.19 | convolution fusion | flops 5874954 | bytes 475200 | tf_op jit(solution)/shard_map/ihqk,ikhd->iqhd/dot_general | solution.py:99
  102.0 17.0 %all_gather.17 = bf16[8,25,1920]{2,1,0:T(8,128)(2,1)S(1)} all-gather(bf16[1,25,1920]{2,1,0:T(8,128)(2,1)S(1)} %convert_element_type.264), channel_id=1, replica_groups=mesh['section'=4,'tp'=8] {'tp'}, dimensions={0}, use_global_device_ids=true | all-gather | bytes 864000 | tf_op jit(solution)/shard_map/all_gather | solution.py:107
  119.0 2.3 convolution_convert_fusion.5
  121.2 5.2 %all-to-all-start.2 = ((bf16[8,25,240]{2,1,0:T(8,128)(2,1)}), bf16[8,25,240]{2,1,0:T(8,128)(2,1)S(1)}, u32[]{:S(2)}, u32[]{:S(2)}) async-start(bf16[8,25,240]{2,1,0:T(8,128)(2,1)} %convolution_convert_fusion.5), calls=%async_computation.2 | async-start | bytes 262144 | tf_op jit(solution)/shard_map/all_to_all | solution.py:190
  126.7 6.5 %all-to-all-done.2 = bf16[8,25,240]{2,1,0:T(8,128)(2,1)S(1)} async-done(((bf16[8,25,240]{2,1,0:T(8,128)(2,1)}), bf16[8,25,240]{2,1,0:T(8,128)(2,1)S(1)}, u32[]{:S(2)}, u32[]{:S(2)}) %all-to-all-start.2) | async-done | bytes 96032 | tf_op jit(solution)/shard_map/all_to_all | solution.py:190
  133.6 3.4 %collective-permute-start = (bf16[1,25,1920]{2,1,0:T(8,128)(2,1)S(1)}, bf16[1,25,1920]{2,1,0:T(8,128)(2,1)S(1)}, u32[]{:S(2)}, u32[]{:S(2)}) collective-permute-start(bf16[1,25,1920]{2,1,0:T(8,128)(2,1)S(1)} %fusion.44), channel_id=1, source_target_pairs={{0,8},{8,16},{16,24},{1,9},{9,17},{17,25},{2,10},{10,18},{18,26},{... | collective-permute-start | bytes 288008 | tf_op jit(solution)/shard_map/ppermute | solution.py:15
  137.6 3.6 %collective-permute-done = bf16[1,25,1920]{2,1,0:T(8,128)(2,1)S(1)} collective-permute-done((bf16[1,25,1920]{2,1,0:T(8,128)(2,1)S(1)}, bf16[1,25,1920]{2,1,0:T(8,128)(2,1)S(1)}, u32[]{:S(2)}, u32[]{:S(2)}) %collective-permute-start) | collective-permute-done | bytes 96032 | tf_op jit(solution)/shard_map/ppermute | solution.py:15
  141.2 1.3 fusion.74
  142.9 16.3 %all_gather.18 = bf16[8,25,1920]{2,1,0:T(8,128)(2,1)S(1)} all-gather(bf16[1,25,1920]{2,1,0:T(8,128)(2,1)S(1)} %add_convert_fusion.1), channel_id=1, replica_groups=mesh['section'=4,'tp'=8] {'tp'}, dimensions={0}, use_global_device_ids=true | all-gather | bytes 864000 | tf_op jit(solution)/shard_map/all_gather | solution.py:179
  159.2 1.8 convolution_convert_fusion
  161.0 2.4 reshape.1151
  163.4 1.8 copy.187
  165.2 4.3 %all-to-all-start.3 = ((bf16[8,25,3,240]{3,1,2,0:T(8,128)(2,1)}), bf16[8,25,3,240]{3,1,2,0:T(8,128)(2,1)}, u32[]{:S(2)}, u32[]{:S(2)}) async-start(bf16[8,25,3,240]{3,1,2,0:T(8,128)(2,1)} %copy.187), calls=%async_computation.3 | async-start | bytes 786432 | tf_op jit(solution)/shard_map/all_to_all | solution.py:74
  169.5 2.0 reshape.1119
  171.5 2.1 copy.193
  174.5 1.7 copy.189
  177.1 4.7 %all-to-all-done.3 = bf16[8,25,3,240]{3,1,2,0:T(8,128)(2,1)} async-done(((bf16[8,25,3,240]{3,1,2,0:T(8,128)(2,1)}), bf16[8,25,3,240]{3,1,2,0:T(8,128)(2,1)}, u32[]{:S(2)}, u32[]{:S(2)}) %all-to-all-start.3) | async-done | bytes 288032 | tf_op jit(solution)/shard_map/all_to_all | solution.py:74
  181.8 1.9 copy.188
  183.7 1.4 all_to_all.65
  186.8 1.9 mul.431
  189.9 1.9 reshape_squeeze.39
  191.8 1.9 reshape_squeeze.40
  196.4 1.3 copy_multiply_fusion
  198.8 2.7 %fusion.27 = f32[30,25,55]{2,1,0:T(8,128)S(1)} fusion(f32[1,25,30,64]{3,1,2,0:T(8,128)S(1)} %copy_multiply_fusion, f32[1,30,30,64]{3,1,2,0:T(8,128)} %copy.193, f32[25,30,64]{2,1,0:T(8,128)S(1)} %multiply_multiply_fusion), kind=kOutput, calls=%fused_computation.35 | convolution fusion | flops 31785600 | bytes 779400 | tf_op jit(solution)/shard_map/iqhd,ikhd->ihqk/dot_general | solution.py:95
  203.6 3.8 %fusion.13 = bf16[1,25,30,64]{3,1,2,0:T(8,128)(2,1)} fusion(bf16[1,25,30,64]{3,1,2,0:T(8,128)(2,1)} %copy.190, bf16[1,30,30,64]{3,1,2,0:T(8,128)(2,1)} %copy.189, f32[30,25]{1,0:T(8,128)S(1)} %fusion.75, f32[30,25,55]{2,1,0:T(8,128)} %copy-done.5), kind=kOutput, calls=%fused_computation.20 | convolution fusion | flops 5874954 | bytes 475200 | tf_op jit(solution)/shard_map/ihqk,ikhd->iqhd/dot_general | solution.py:99
  207.4 1.7 copy.195
  210.3 16.2 %all_gather.19 = bf16[8,25,1920]{2,1,0:T(8,128)(2,1)S(1)} all-gather(bf16[1,25,1920]{2,1,0:T(8,128)(2,1)S(1)} %convert_element_type.289), channel_id=1, replica_groups=mesh['section'=4,'tp'=8] {'tp'}, dimensions={0}, use_global_device_ids=true | all-gather | bytes 864000 | tf_op jit(solution)/shard_map/all_gather | solution.py:107
  226.5 2.3 convolution_convert_fusion.4
  228.8 4.0 %all-to-all-start.4 = ((bf16[8,25,240]{2,1,0:T(8,128)(2,1)}), bf16[8,25,240]{2,1,0:T(8,128)(2,1)}, u32[]{:S(2)}, u32[]{:S(2)}) async-start(bf16[8,25,240]{2,1,0:T(8,128)(2,1)} %convolution_convert_fusion.4), calls=%async_computation.4 | async-start | bytes 262144 | tf_op jit(solution)/shard_map/all_to_all | solution.py:190
  233.5 6.1 %all-to-all-done.4 = bf16[8,25,240]{2,1,0:T(8,128)(2,1)} async-done(((bf16[8,25,240]{2,1,0:T(8,128)(2,1)}), bf16[8,25,240]{2,1,0:T(8,128)(2,1)}, u32[]{:S(2)}, u32[]{:S(2)}) %all-to-all-start.4) | async-done | bytes 96032 | tf_op jit(solution)/shard_map/all_to_all | solution.py:190
  (142 shorter events, 44.2 us)
Async XLA Ops:
  0.0 53.6 %copy-start = (bf16[1,1920,3,240]{1,3,2,0:T(8,128)(2,1)S(1)}, bf16[1,1920,3,240]{1,3,2,0:T(8,128)(2,1)}, u32[]{:S(2)}) copy-start(bf16[1,1920,3,240]{1,3,2,0:T(8,128)(2,1)} %param.23) | copy-start | bytes 8294404
  2.2 26.7 %copy-start.3 = (bf16[1,1,25,1920]{3,2,1,0:T(8,128)(2,1)S(1)}, bf16[1,1,25,1920]{3,2,1,0:T(8,128)(2,1)}, u32[]{:S(2)}) copy-start(bf16[1,1,25,1920]{3,2,1,0:T(8,128)(2,1)} %param.14) | copy-start | bytes 288004
  2.8 26.5 %copy-start.7 = (bf16[1,2,1,30,1920]{4,1,3,2,0:T(2,128)(2,1)S(1)}, bf16[1,2,1,30,1920]{4,1,3,2,0:T(2,128)(2,1)}, u32[]{:S(2)}) copy-start(bf16[1,2,1,30,1920]{4,1,3,2,0:T(2,128)(2,1)} %param.26) | copy-start | bytes 691204
  23.7 11.5 %all-to-all-start = ((f32[1,2,8,3,240]{4,1,3,0,2:T(2,128)}), f32[1,2,8,3,240]{4,1,3,0,2:T(2,128)S(1)}, u32[]{:S(2)}, u32[]{:S(2)}) async-start(f32[1,2,8,3,240]{4,1,3,0,2:T(2,128)} %copy.165), calls=%async_computation | async-start | bytes 98304 | tf_op jit(solution)/shard_map/all_to_all | solution.py:155
  58.0 18.7 %all-to-all-start.1 = ((bf16[8,25,3,240]{3,1,2,0:T(8,128)(2,1)}), bf16[8,25,3,240]{3,1,2,0:T(8,128)(2,1)}, u32[]{:S(2)}, u32[]{:S(2)}) async-start(bf16[8,25,3,240]{3,1,2,0:T(8,128)(2,1)} %copy.169), calls=%async_computation.1 | async-start | bytes 786432 | tf_op jit(solution)/shard_map/all_to_all | solution.py:74
  64.0 6.7 %copy-start.9 = (f32[5,5,3,3]{1,0,3,2:T(8,128)S(1)}, f32[5,5,3,3]{1,0,3,2:T(8,128)}, u32[]{:S(2)}) copy-start(f32[5,5,3,3]{1,0,3,2:T(8,128)} %broadcast_multiply_fusion.1) | copy-start | bytes 2704
  64.0 7.5 %copy-start.12 = (f32[5,5,2,2]{1,0,3,2:T(8,128)S(1)}, f32[5,5,2,2]{1,0,3,2:T(8,128)}, u32[]{:S(2)}) copy-start(f32[5,5,2,2]{1,0,3,2:T(8,128)} %broadcast_multiply_fusion.2) | copy-start | bytes 1204
  64.0 8.3 %copy-start.19 = (f32[5]{0:T(128)S(1)}, f32[5]{0:T(128)}, u32[]{:S(2)}) copy-start(f32[5]{0:T(128)} %maximum_multiply_fusion.3) | copy-start | bytes 64
  64.0 12.7 %copy-start.20 = (f32[1,30]{1,0:T(1,128)S(1)}, f32[1,30]{1,0:T(1,128)}, u32[]{:S(2)}) copy-start(f32[1,30]{1,0:T(1,128)} %param.25) | copy-start | bytes 364
  78.4 9.8 %copy-start.1 = (bf16[1,25,3,1920]{3,1,2,0:T(8,128)(2,1)}, bf16[1,25,3,1920]{3,1,2,0:T(8,128)(2,1)S(1)}, u32[]{:S(2)}) copy-start(bf16[1,25,3,1920]{3,1,2,0:T(8,128)(2,1)S(1)} %all_to_all.60) | copy-start | bytes 864004
  90.0 4.6 %slice-start = ((bf16[1,25,3,1920]{3,1,2,0:T(8,128)(2,1)}), bf16[1,25,1,1920]{3,1,2,0:T(8,128)(2,1)S(1)}, s32[]{:S(2)}) async-start(bf16[1,25,3,1920]{3,1,2,0:T(8,128)(2,1)} %copy-done.1), calls=%async_computation.5 | async-start | bytes 245760 | tf_op jit(solution)/shard_map/slice | solution.py:80
  100.6 25.8 %copy-start.13 = (f32[30,32]{1,0:T(8,128)S(1)}, f32[30,32]{1,0:T(8,128)}, u32[]{:S(2)}) copy-start(f32[30,32]{1,0:T(8,128)} %gather_fusion.1) | copy-start | bytes 11524
  100.6 25.8 %copy-start.14 = (f32[25,9]{1,0:T(8,128)S(1)}, f32[25,9]{1,0:T(8,128)}, u32[]{:S(2)}) copy-start(f32[25,9]{1,0:T(8,128)} %copy.183) | copy-start | bytes 2704
  100.6 25.8 %copy-start.15 = (f32[25,4]{1,0:T(8,128)S(1)}, f32[25,4]{1,0:T(8,128)}, u32[]{:S(2)}) copy-start(f32[25,4]{1,0:T(8,128)} %copy.182) | copy-start | bytes 1204
  100.6 25.8 %copy-start.16 = (f32[25,1]{1,0:T(8,128)S(1)}, f32[25,1]{1,0:T(8,128)}, u32[]{:S(2)}) copy-start(f32[25,1]{1,0:T(8,128)} %copy.181) | copy-start | bytes 304
  100.6 25.8 %copy-start.17 = (f32[25,16]{1,0:T(8,128)S(1)}, f32[25,16]{1,0:T(8,128)}, u32[]{:S(2)}) copy-start(f32[25,16]{1,0:T(8,128)} %mul.419) | copy-start | bytes 4804
  100.7 32.9 %copy-start.4 = (bf16[1,1,25,1920]{3,2,1,0:T(8,128)(2,1)S(1)}, bf16[1,1,25,1920]{3,2,1,0:T(8,128)(2,1)}, u32[]{:S(2)}) copy-start(bf16[1,1,25,1920]{3,2,1,0:T(8,128)(2,1)} %param.14) | copy-start | bytes 288004
  100.7 32.9 %copy-start.11 = (f32[1920]{0:T(1024)S(1)}, f32[1920]{0:T(1024)}, u32[]{:S(2)}) copy-start(f32[1920]{0:T(1024)} %get-tuple-element.12) | copy-start | bytes 23044
  101.8 35.2 %copy-start.10 = (f32[1,3,1920]{2,0,1:T(1,128)S(1)}, f32[1,3,1920]{2,0,1:T(1,128)}, u32[]{:S(2)}) copy-start(f32[1,3,1920]{2,0,1:T(1,128)} %get-tuple-element.21) | copy-start | bytes 69124
  121.2 11.9 %all-to-all-start.2 = ((bf16[8,25,240]{2,1,0:T(8,128)(2,1)}), bf16[8,25,240]{2,1,0:T(8,128)(2,1)S(1)}, u32[]{:S(2)}, u32[]{:S(2)}) async-start(bf16[8,25,240]{2,1,0:T(8,128)(2,1)} %convolution_convert_fusion.5), calls=%async_computation.2 | async-start | bytes 262144 | tf_op jit(solution)/shard_map/all_to_all | solution.py:190
  133.6 7.7 %collective-permute-start = (bf16[1,25,1920]{2,1,0:T(8,128)(2,1)S(1)}, bf16[1,25,1920]{2,1,0:T(8,128)(2,1)S(1)}, u32[]{:S(2)}, u32[]{:S(2)}) collective-permute-start(bf16[1,25,1920]{2,1,0:T(8,128)(2,1)S(1)} %fusion.44), channel_id=1, source_target_pairs={{0,8},{8,16},{16,24},{1,9},{9,17},{17,25},{2,10},{10,18},{18,26},{... | collective-permute-start | bytes 288008 | tf_op jit(solution)/shard_map/ppermute | solution.py:15
  161.0 12.6 %copy-start.8 = (bf16[30,1920]{1,0:T(8,128)(2,1)S(1)}, bf16[30,1920]{1,0:T(8,128)(2,1)}, u32[]{:S(2)}) copy-start(bf16[30,1920]{1,0:T(8,128)(2,1)} %get-tuple-element.7) | copy-start | bytes 345604
  165.2 16.6 %all-to-all-start.3 = ((bf16[8,25,3,240]{3,1,2,0:T(8,128)(2,1)}), bf16[8,25,3,240]{3,1,2,0:T(8,128)(2,1)}, u32[]{:S(2)}, u32[]{:S(2)}) async-start(bf16[8,25,3,240]{3,1,2,0:T(8,128)(2,1)} %copy.187), calls=%async_computation.3 | async-start | bytes 786432 | tf_op jit(solution)/shard_map/all_to_all | solution.py:74
  185.2 9.7 %copy-start.2 = (bf16[1,25,3,1920]{3,1,2,0:T(8,128)(2,1)}, bf16[1,25,3,1920]{3,1,2,0:T(8,128)(2,1)S(1)}, u32[]{:S(2)}) copy-start(bf16[1,25,3,1920]{3,1,2,0:T(8,128)(2,1)S(1)} %all_to_all.65) | copy-start | bytes 864004
  195.5 7.1 %slice-start.1 = ((bf16[1,25,3,1920]{3,1,2,0:T(8,128)(2,1)}), bf16[1,25,1,1920]{3,1,2,0:T(8,128)(2,1)S(1)}, s32[]{:S(2)}) async-start(bf16[1,25,3,1920]{3,1,2,0:T(8,128)(2,1)} %copy-done.2), calls=%async_computation.6 | async-start | bytes 245760 | tf_op jit(solution)/shard_map/slice | solution.py:80
  201.5 0.8 copy-start.5
  207.4 25.4 %copy-start.6 = (f32[1,1,25,1920]{3,2,1,0:T(8,128)S(1)}, f32[1,1,25,1920]{3,2,1,0:T(8,128)}, u32[]{:S(2)}) copy-start(f32[1,1,25,1920]{3,2,1,0:T(8,128)} %reshape.1149) | copy-start | bytes 576004
  209.2 33.2 %copy-start.18 = (f32[1920]{0:T(1024)S(1)}, f32[1920]{0:T(1024)}, u32[]{:S(2)}) copy-start(f32[1920]{0:T(1024)} %get-tuple-element.9) | copy-start | bytes 23044
  228.8 10.8 %all-to-all-start.4 = ((bf16[8,25,240]{2,1,0:T(8,128)(2,1)}), bf16[8,25,240]{2,1,0:T(8,128)(2,1)}, u32[]{:S(2)}, u32[]{:S(2)}) async-start(bf16[8,25,240]{2,1,0:T(8,128)(2,1)} %convolution_convert_fusion.4), calls=%async_computation.4 | async-start | bytes 262144 | tf_op jit(solution)/shard_map/all_to_all | solution.py:190
where the time goes:
time: 246 us; the launch traced here: 244 us
  blocking collectives  82.9 us (34%)
  local copies, waits for them, and re-layouts  63.8 us (26%)
  starting transfers between devices  27.2 us (11%)
  matrix products  25.3 us (10%)
  other arithmetic  23.5 us (10%)
  waiting for transfers between devices  20.9 us (8%)
    all_gather x2, blocking collectives, local(): lax.all_gather(normed, 'tp', axis=0, tiled=True)  33.3 us
    all_gather x2, blocking collectives, project_out(): lax.all_gather(attended, 'tp', axis=0, tiled=True)  33.2 us
    all_gather x1, blocking collectives, local(): gated_response = lax.all_gather(activated_part, 'tp', axis=2, tiled=True)  16.4 us
    all_to_all x2, waiting for transfers between devices, local(): lax.all_to_all(projected_cols, 'tp', split_axis=0, concat_axis=2, tiled=T...  12.5 us
    all_to_all x2, starting transfers between devices, attention(): lax.all_to_all(qkv_cols, 'tp', split_axis=0, concat_axis=3, tiled=True)  9.52 us
    all_to_all x2, starting transfers between devices, local(): lax.all_to_all(projected_cols, 'tp', split_axis=0, concat_axis=2, tiled=T...  9.2 us
    dot_general x2, matrix products, attention(): jnp.einsum('ihqk,ikhd->iqhd', probabilities, all_values, preferred_elemen...  7.32 us
    reshape x4, local copies, waits for them, and re-layouts, local(): qkv_cols.reshape(qkv_cols.shape[0], qkv_cols.shape[1], 3, column_width)  6.8 us
  transfers between devices with their start and end apart: 6, of which 4 were waited for; matrix products, arithmetic and copies ran while one was open for 12% of the time, Pallas kernels for 0%

commit v1 on v0

--- a/solution.py
+++ b/solution.py
@@ -103,11 +103,14 @@
 
 
 def project_out(attended, out_matrix):
-    return jnp.dot(
-        lax.all_gather(attended, "tp", axis=0, tiled=True),
-        out_matrix,
-        preferred_element_type=jnp.float32,
-    )
+
+    def answer_bands(a0):
+        inter = jnp.stack([a0 for _ in range(lax.axis_size("tp"))])
+        n_now = lax.all_to_all(inter, "tp", 0, 0)
+        later = jnp.concatenate(n_now, 0)
+        return later
+
+    return jnp.dot(answer_bands(attended), out_matrix, preferred_element_type=jnp.float32)
 
 
 def pass_on(latent_stream):

time: 246 us -> 275 us (1.12)
  waiting for transfers between devices: 20.9 us -> 79.1 us
  blocking collectives: 82.9 us -> 49.7 us
  starting transfers between devices: 27.2 us -> 34 us
  local copies, waits for them, and re-layouts: 63.8 us -> 59.7 us
    all_to_all x0 -> x2, waiting for transfers between devices: none -> 45.5 us  [answer_bands(): n_now = lax.all_to_all(inter, 'tp', 0, 0)]
    all_gather x2 -> x0, blocking collectives: 33.2 us -> none  [project_out(): lax.all_gather(attended, 'tp', axis=0, tiled=True)]
    all_to_all x2, waiting for transfers between devices: 4.72 us -> 18.4 us  [attention(): lax.all_to_all(qkv_cols, 'tp', split_axis=0, concat_axis=3, tiled=True)]
    all_to_all x0 -> x2, starting transfers between devices: none -> 8.6 us  [answer_bands(): n_now = lax.all_to_all(inter, 'tp', 0, 0)]
    unnamed x45 -> x49, local copies, waits for them, and re-layouts: 5.77 us -> 5.82 us
  transfers between devices with their start and end apart: 6 -> 8, of which waited for: 4 -> 7; matrix products, arithmetic and copies ran while one was open for 12% -> 9% of each run, Pallas kernels for 0% -> 0%
where the time goes in v1:
time: 275 us; the launch traced here: 273 us
  waiting for transfers between devices  79.1 us (29%)
  local copies, waits for them, and re-layouts  59.7 us (22%)
  blocking collectives  49.7 us (18%)
  starting transfers between devices  34 us (12%)
  matrix products  26.6 us (10%)
  other arithmetic  23.1 us (8%)
    all_to_all x2, waiting for transfers between devices, answer_bands(): n_now = lax.all_to_all(inter, 'tp', 0, 0)  45.5 us
    all_gather x2, blocking collectives, local(): lax.all_gather(normed, 'tp', axis=0, tiled=True)  33.3 us
    all_to_all x2, waiting for transfers between devices, attention(): lax.all_to_all(qkv_cols, 'tp', split_axis=0, concat_axis=3, tiled=True)  18.4 us
    all_gather x1, blocking collectives, local(): gated_response = lax.all_gather(activated_part, 'tp', axis=2, tiled=True)  16.4 us
    all_to_all x2, waiting for transfers between devices, local(): lax.all_to_all(projected_cols, 'tp', split_axis=0, concat_axis=2, tiled=T...  11 us
    all_to_all x2, starting transfers between devices, attention(): lax.all_to_all(qkv_cols, 'tp', split_axis=0, concat_axis=3, tiled=True)  9.52 us
    all_to_all x2, starting transfers between devices, answer_bands(): n_now = lax.all_to_all(inter, 'tp', 0, 0)  8.6 us
    all_to_all x2, starting transfers between devices, local(): lax.all_to_all(projected_cols, 'tp', split_axis=0, concat_axis=2, tiled=T...  7.37 us
  transfers between devices with their start and end apart: 8, of which 7 were waited for; matrix products, arithmetic and copies ran while one was open for 9% of the time, Pallas kernels for 0%

profile of v1, /device:TPU:4, one launch (start us, length us, event | category | flops | bytes accessed | tf_op | source)
XLA Modules:
  0.0 272.7 jit_solution(7386561358345846522)
XLA Ops:
  3.0 16.4 %all_gather.9 = bf16[2,8,1920]{1,0,2:T(2,128)(2,1)S(1)} all-gather(bf16[2,8,240]{1,0,2:T(2,128)(2,1)S(1)} %copy.163), channel_id=1, replica_groups=mesh['section'=4,'tp'=8] {'tp'}, dimensions={2}, use_global_device_ids=true | all-gather | bytes 69120 | tf_op jit(solution)/shard_map/all_gather | solution.py:147
  20.2 2.9 %fusion.17 = f32[1,2,8,3,240]{4,2,3,1,0:T(8,128)S(1)} fusion(bf16[1,1920,3,240]{1,3,2,0:T(8,128)(2,1)} %param.21, bf16[2,8,1920,1]{1,0,2,3:T(2,128)(2,1)S(1)} %bitcast.182, f32[3,240]{1,0:T(4,128)S(1)} %bitcast.185), kind=kOutput, calls=%fused_computation.24 | convolution fusion | flops 44248320 | bytes 2875200 | tf_op jit(solution)/shard_map/dot_general | solution.py:151
  23.7 5.1 %all-to-all-start = ((f32[1,2,8,3,240]{4,1,3,0,2:T(2,128)}), f32[1,2,8,3,240]{4,1,3,0,2:T(2,128)S(1)}, u32[]{:S(2)}, u32[]{:S(2)}) async-start(f32[1,2,8,3,240]{4,1,3,0,2:T(2,128)} %copy.165), calls=%async_computation | async-start | bytes 98304 | tf_op jit(solution)/shard_map/all_to_all | solution.py:158
  29.8 1.9 convert_reduce_fusion.1
  31.8 1.6 slice_reduce_fusion
  36.7 3.0 %copy.180 = f32[4096,32]{1,0:T(8,128)} copy(f32[4096,32]{0,1:T(8,128)} %param.17) | data formatting | bytes 1048576 | tf_op args[3]
  40.7 17.0 %all_gather.10 = bf16[8,25,1920]{2,1,0:T(8,128)(2,1)S(1)} all-gather(bf16[1,25,1920]{2,1,0:T(8,128)(2,1)S(1)} %fusion.45), channel_id=1, replica_groups=mesh['section'=4,'tp'=8] {'tp'}, dimensions={0}, use_global_device_ids=true | all-gather | bytes 864000 | tf_op jit(solution)/shard_map/all_gather | solution.py:182
  57.6 1.8 convolution_convert_fusion.1
  59.4 1.7 reshape.1154
  62.0 5.2 %all-to-all-start.1 = ((bf16[8,25,3,240]{3,1,2,0:T(8,128)(2,1)}), bf16[8,25,3,240]{3,1,2,0:T(8,128)(2,1)S(1)}, u32[]{:S(2)}, u32[]{:S(2)}) async-start(bf16[8,25,3,240]{3,1,2,0:T(8,128)(2,1)} %copy.169), calls=%async_computation.1 | async-start | bytes 786432 | tf_op jit(solution)/shard_map/all_to_all | solution.py:74
  68.5 11.2 %all-to-all-done.1 = bf16[8,25,3,240]{3,1,2,0:T(8,128)(2,1)S(1)} async-done(((bf16[8,25,3,240]{3,1,2,0:T(8,128)(2,1)}), bf16[8,25,3,240]{3,1,2,0:T(8,128)(2,1)S(1)}, u32[]{:S(2)}, u32[]{:S(2)}) %all-to-all-start.1) | async-done | bytes 288032 | tf_op jit(solution)/shard_map/all_to_all | solution.py:74
  84.2 1.4 copy.173
  85.6 1.8 copy_multiply_fusion.1
  88.5 1.7 slice_multiply_fusion.1
  90.1 1.9 mul.390
  93.5 2.8 %fusion.26 = f32[30,25,55]{2,1,0:T(8,128)S(1)} fusion(f32[1,25,30,64]{3,1,2,0:T(8,128)} %copy_multiply_fusion.1, f32[1,30,30,64]{3,1,2,0:T(8,128)} %copy.175, f32[25,30,64]{2,1,0:T(8,128)S(1)} %multiply_multiply_fusion.1), kind=kOutput, calls=%fused_computation.33 | convolution fusion | flops 31785600 | bytes 779400 | tf_op jit(solution)/shard_map/iqhd,ikhd->ihqk/dot_general | solution.py:95
  97.5 1.7 copy.172
  99.2 3.5 %fusion.12 = bf16[1,25,30,64]{3,1,2,0:T(8,128)(2,1)} fusion(bf16[1,25,30,64]{3,1,2,0:T(8,128)(2,1)} %copy.172, bf16[1,30,30,64]{3,1,2,0:T(8,128)(2,1)} %copy.171, f32[30,25]{1,0:T(8,128)S(1)} %fusion.75, f32[30,25,55]{2,1,0:T(8,128)S(1)} %fusion.26), kind=kOutput, calls=%fused_computation.19 | convolution fusion | flops 5874954 | bytes 475200 | tf_op jit(solution)/shard_map/ihqk,ikhd->iqhd/dot_general | solution.py:99
  105.0 4.4 %all-to-all-start.2 = ((bf16[8,1,25,1920]{3,2,1,0:T(8,128)(2,1)}), bf16[8,1,25,1920]{3,2,1,0:T(8,128)(2,1)}, u32[]{:S(2)}, u32[]{:S(2)}) async-start(bf16[8,1,25,1920]{3,2,1,0:T(8,128)(2,1)} %stack.11), calls=%async_computation.2 | async-start | bytes 1966080 | tf_op jit(solution)/shard_map/all_to_all | solution.py:109
  111.2 2.2 gather_fusion.1
  113.3 21.2 %all-to-all-done.2 = bf16[8,1,25,1920]{3,2,1,0:T(8,128)(2,1)} async-done(((bf16[8,1,25,1920]{3,2,1,0:T(8,128)(2,1)}), bf16[8,1,25,1920]{3,2,1,0:T(8,128)(2,1)}, u32[]{:S(2)}, u32[]{:S(2)}) %all-to-all-start.2) | async-done | bytes 768032 | tf_op jit(solution)/shard_map/all_to_all | solution.py:109
  134.5 2.6 convolution_convert_fusion.5
  137.1 3.4 %all-to-all-start.3 = ((bf16[8,25,240]{2,1,0:T(8,128)(2,1)}), bf16[8,25,240]{2,1,0:T(8,128)(2,1)S(1)}, u32[]{:S(2)}, u32[]{:S(2)}) async-start(bf16[8,25,240]{2,1,0:T(8,128)(2,1)} %convolution_convert_fusion.5), calls=%async_computation.3 | async-start | bytes 262144 | tf_op jit(solution)/shard_map/all_to_all | solution.py:193
  141.3 5.8 %all-to-all-done.3 = bf16[8,25,240]{2,1,0:T(8,128)(2,1)S(1)} async-done(((bf16[8,25,240]{2,1,0:T(8,128)(2,1)}), bf16[8,25,240]{2,1,0:T(8,128)(2,1)S(1)}, u32[]{:S(2)}, u32[]{:S(2)}) %all-to-all-start.3) | async-done | bytes 96032 | tf_op jit(solution)/shard_map/all_to_all | solution.py:193
  147.6 3.4 %collective-permute-start = (bf16[1,25,1920]{2,1,0:T(8,128)(2,1)S(1)}, bf16[1,25,1920]{2,1,0:T(8,128)(2,1)S(1)}, u32[]{:S(2)}, u32[]{:S(2)}) collective-permute-start(bf16[1,25,1920]{2,1,0:T(8,128)(2,1)S(1)} %fusion.46), channel_id=1, source_target_pairs={{0,8},{8,16},{16,24},{1,9},{9,17},{17,25},{2,10},{10,18},{18,26},{... | collective-permute-start | bytes 288008 | tf_op jit(solution)/shard_map/ppermute | solution.py:15
  151.0 4.2 %collective-permute-done = bf16[1,25,1920]{2,1,0:T(8,128)(2,1)S(1)} collective-permute-done((bf16[1,25,1920]{2,1,0:T(8,128)(2,1)S(1)}, bf16[1,25,1920]{2,1,0:T(8,128)(2,1)S(1)}, u32[]{:S(2)}, u32[]{:S(2)}) %collective-permute-start) | collective-permute-done | bytes 96032 | tf_op jit(solution)/shard_map/ppermute | solution.py:15
  156.9 16.3 %all_gather.11 = bf16[8,25,1920]{2,1,0:T(8,128)(2,1)S(1)} all-gather(bf16[1,25,1920]{2,1,0:T(8,128)(2,1)S(1)} %add_convert_fusion.1), channel_id=1, replica_groups=mesh['section'=4,'tp'=8] {'tp'}, dimensions={0}, use_global_device_ids=true | all-gather | bytes 864000 | tf_op jit(solution)/shard_map/all_gather | solution.py:182
  173.2 1.8 convolution_convert_fusion
  175.0 2.4 reshape.1157
  177.4 1.8 copy.187
  179.2 4.3 %all-to-all-start.4 = ((bf16[8,25,3,240]{3,1,2,0:T(8,128)(2,1)}), bf16[8,25,3,240]{3,1,2,0:T(8,128)(2,1)}, u32[]{:S(2)}, u32[]{:S(2)}) async-start(bf16[8,25,3,240]{3,1,2,0:T(8,128)(2,1)} %copy.187), calls=%async_computation.4 | async-start | bytes 786432 | tf_op jit(solution)/shard_map/all_to_all | solution.py:74
  183.6 2.0 reshape.1125
  185.5 2.1 copy.193
  188.6 7.2 %all-to-all-done.4 = bf16[8,25,3,240]{3,1,2,0:T(8,128)(2,1)} async-done(((bf16[8,25,3,240]{3,1,2,0:T(8,128)(2,1)}), bf16[8,25,3,240]{3,1,2,0:T(8,128)(2,1)}, u32[]{:S(2)}, u32[]{:S(2)}) %all-to-all-start.4) | async-done | bytes 288032 | tf_op jit(solution)/shard_map/all_to_all | solution.py:74
  195.9 1.9 copy.188
  197.8 1.4 all_to_all.72
  200.8 1.9 mul.431
  203.9 1.9 reshape_squeeze.39
  205.8 1.9 reshape_squeeze.40
  212.8 2.7 fusion.29
  217.6 3.9 %fusion.13 = bf16[1,25,30,64]{3,1,2,0:T(8,128)(2,1)} fusion(bf16[1,25,30,64]{3,1,2,0:T(8,128)(2,1)} %copy.190, bf16[1,30,30,64]{3,1,2,0:T(8,128)(2,1)} %copy.189, f32[30,25]{1,0:T(8,128)S(1)} %fusion.77, f32[30,25,55]{2,1,0:T(8,128)} %copy-done.5), kind=kOutput, calls=%fused_computation.20 | convolution fusion | flops 5874954 | bytes 475200 | tf_op jit(solution)/shard_map/ihqk,ikhd->iqhd/dot_general | solution.py:99
  221.5 1.7 copy.195
  225.3 4.2 %all-to-all-start.5 = ((bf16[8,1,25,1920]{3,2,1,0:T(8,128)(2,1)}), bf16[8,1,25,1920]{3,2,1,0:T(8,128)(2,1)}, u32[]{:S(2)}, u32[]{:S(2)}) async-start(bf16[8,1,25,1920]{3,2,1,0:T(8,128)(2,1)} %stack.12), calls=%async_computation.5 | async-start | bytes 1966080 | tf_op jit(solution)/shard_map/all_to_all | solution.py:109
  230.4 24.3 %all-to-all-done.5 = bf16[8,1,25,1920]{3,2,1,0:T(8,128)(2,1)} async-done(((bf16[8,1,25,1920]{3,2,1,0:T(8,128)(2,1)}), bf16[8,1,25,1920]{3,2,1,0:T(8,128)(2,1)}, u32[]{:S(2)}, u32[]{:S(2)}) %all-to-all-start.5) | async-done | bytes 768032 | tf_op jit(solution)/shard_map/all_to_all | solution.py:109
  254.7 2.6 convolution_convert_fusion.4
  257.3 4.0 %all-to-all-start.6 = ((bf16[8,25,240]{2,1,0:T(8,128)(2,1)}), bf16[8,25,240]{2,1,0:T(8,128)(2,1)}, u32[]{:S(2)}, u32[]{:S(2)}) async-start(bf16[8,25,240]{2,1,0:T(8,128)(2,1)} %convolution_convert_fusion.4), calls=%async_computation.6 | async-start | bytes 262144 | tf_op jit(solution)/shard_map/all_to_all | solution.py:193
  261.3 1.6 fusion.47
  263.0 5.1 %all-to-all-done.6 = bf16[8,25,240]{2,1,0:T(8,128)(2,1)} async-done(((bf16[8,25,240]{2,1,0:T(8,128)(2,1)}), bf16[8,25,240]{2,1,0:T(8,128)(2,1)}, u32[]{:S(2)}, u32[]{:S(2)}) %all-to-all-start.6) | async-done | bytes 96032 | tf_op jit(solution)/shard_map/all_to_all | solution.py:193
  (150 shorter events, 45.5 us)
Async XLA Ops:
  0.0 57.6 %copy-start = (bf16[1,1920,3,240]{1,3,2,0:T(8,128)(2,1)S(1)}, bf16[1,1920,3,240]{1,3,2,0:T(8,128)(2,1)}, u32[]{:S(2)}) copy-start(bf16[1,1920,3,240]{1,3,2,0:T(8,128)(2,1)} %param.23) | copy-start | bytes 8294404
  2.2 26.7 %copy-start.3 = (bf16[1,1,25,1920]{3,2,1,0:T(8,128)(2,1)S(1)}, bf16[1,1,25,1920]{3,2,1,0:T(8,128)(2,1)}, u32[]{:S(2)}) copy-start(bf16[1,1,25,1920]{3,2,1,0:T(8,128)(2,1)} %param.14) | copy-start | bytes 288004
  2.8 27.0 %copy-start.8 = (bf16[1,2,1,30,1920]{4,1,3,2,0:T(2,128)(2,1)S(1)}, bf16[1,2,1,30,1920]{4,1,3,2,0:T(2,128)(2,1)}, u32[]{:S(2)}) copy-start(bf16[1,2,1,30,1920]{4,1,3,2,0:T(2,128)(2,1)} %param.26) | copy-start | bytes 691204
  19.5 12.3 %copy-start.9 = (bf16[1,2,1,30,1920]{4,1,3,2,0:T(2,128)(2,1)S(1)}, bf16[1,2,1,30,1920]{4,1,3,2,0:T(2,128)(2,1)}, u32[]{:S(2)}) copy-start(bf16[1,2,1,30,1920]{4,1,3,2,0:T(2,128)(2,1)} %param.27) | copy-start | bytes 691204
  23.7 16.0 %all-to-all-start = ((f32[1,2,8,3,240]{4,1,3,0,2:T(2,128)}), f32[1,2,8,3,240]{4,1,3,0,2:T(2,128)S(1)}, u32[]{:S(2)}, u32[]{:S(2)}) async-start(f32[1,2,8,3,240]{4,1,3,0,2:T(2,128)} %copy.165), calls=%async_computation | async-start | bytes 98304 | tf_op jit(solution)/shard_map/all_to_all | solution.py:158
  28.9 4.5 %copy-start.13 = (f32[5]{0:T(128)}, f32[5]{0:T(128)S(1)}, u32[]{:S(2)}) copy-start(f32[5]{0:T(128)S(1)} %get-tuple-element.25) | copy-start | bytes 64
  28.9 4.5 %copy-start.15 = (f32[5]{0:T(128)}, f32[5]{0:T(128)S(1)}, u32[]{:S(2)}) copy-start(f32[5]{0:T(128)S(1)} %get-tuple-element.26) | copy-start | bytes 64
  29.1 4.4 %copy-start.17 = (f32[25]{0:T(128)}, f32[25]{0:T(128)S(1)}, u32[]{:S(2)}) copy-start(f32[25]{0:T(128)S(1)} %broadcast_multiply_fusion.4) | copy-start | bytes 304
  35.6 4.9 %copy-start.18 = (f32[25]{0:T(128)S(1)}, f32[25]{0:T(128)}, u32[]{:S(2)}) copy-start(f32[25]{0:T(128)} %copy-done.17) | copy-start | bytes 304
  35.6 4.9 %copy-start.19 = (f32[25]{0:T(128)S(1)}, f32[25]{0:T(128)}, u32[]{:S(2)}) copy-start(f32[25]{0:T(128)} %add_rsqrt_fusion.5) | copy-start | bytes 304
  57.6 10.9 %copy-start.22 = (f32[1,30]{1,0:T(1,128)S(1)}, f32[1,30]{1,0:T(1,128)}, u32[]{:S(2)}) copy-start(f32[1,30]{1,0:T(1,128)} %param.25) | copy-start | bytes 364
  62.0 17.7 %all-to-all-start.1 = ((bf16[8,25,3,240]{3,1,2,0:T(8,128)(2,1)}), bf16[8,25,3,240]{3,1,2,0:T(8,128)(2,1)S(1)}, u32[]{:S(2)}, u32[]{:S(2)}) async-start(bf16[8,25,3,240]{3,1,2,0:T(8,128)(2,1)} %copy.169), calls=%async_computation.1 | async-start | bytes 786432 | tf_op jit(solution)/shard_map/all_to_all | solution.py:74
  80.4 9.8 %copy-start.1 = (bf16[1,25,3,1920]{3,1,2,0:T(8,128)(2,1)}, bf16[1,25,3,1920]{3,1,2,0:T(8,128)(2,1)S(1)}, u32[]{:S(2)}) copy-start(bf16[1,25,3,1920]{3,1,2,0:T(8,128)(2,1)S(1)} %all_to_all.66) | copy-start | bytes 864004
  92.0 4.6 %slice-start = ((bf16[1,25,3,1920]{3,1,2,0:T(8,128)(2,1)}), bf16[1,25,1,1920]{3,1,2,0:T(8,128)(2,1)S(1)}, s32[]{:S(2)}) async-start(bf16[1,25,3,1920]{3,1,2,0:T(8,128)(2,1)} %copy-done.1), calls=%async_computation.7 | async-start | bytes 245760 | tf_op jit(solution)/shard_map/slice | solution.py:80
  99.2 10.1 %copy-start.14 = (f32[5]{0:T(128)S(1)}, f32[5]{0:T(128)}, u32[]{:S(2)}) copy-start(f32[5]{0:T(128)} %copy-done.13) | copy-start | bytes 64
  99.2 10.1 %copy-start.16 = (f32[5]{0:T(128)S(1)}, f32[5]{0:T(128)}, u32[]{:S(2)}) copy-start(f32[5]{0:T(128)} %copy-done.15) | copy-start | bytes 64
  99.2 10.2 %copy-start.20 = (f32[3]{0:T(128)S(1)}, f32[3]{0:T(128)}, u32[]{:S(2)}) copy-start(f32[3]{0:T(128)} %get-tuple-element.29) | copy-start | bytes 40
  102.7 6.7 %copy-start.21 = (f32[3]{0:T(128)S(1)}, f32[3]{0:T(128)}, u32[]{:S(2)}) copy-start(f32[3]{0:T(128)} %get-tuple-element.30) | copy-start | bytes 40
  103.9 36.6 %copy-start.12 = (f32[25,16]{1,0:T(8,128)S(1)}, f32[25,16]{1,0:T(8,128)}, u32[]{:S(2)}) copy-start(f32[25,16]{1,0:T(8,128)} %mul.419) | copy-start | bytes 4804
  105.0 42.5 %copy-start.4 = (bf16[1,1,25,1920]{3,2,1,0:T(8,128)(2,1)S(1)}, bf16[1,1,25,1920]{3,2,1,0:T(8,128)(2,1)}, u32[]{:S(2)}) copy-start(bf16[1,1,25,1920]{3,2,1,0:T(8,128)(2,1)} %param.14) | copy-start | bytes 288004
  105.0 29.5 %all-to-all-start.2 = ((bf16[8,1,25,1920]{3,2,1,0:T(8,128)(2,1)}), bf16[8,1,25,1920]{3,2,1,0:T(8,128)(2,1)}, u32[]{:S(2)}, u32[]{:S(2)}) async-start(bf16[8,1,25,1920]{3,2,1,0:T(8,128)(2,1)} %stack.11), calls=%async_computation.2 | async-start | bytes 1966080 | tf_op jit(solution)/shard_map/all_to_all | solution.py:109
  109.4 41.6 %copy-start.11 = (f32[1,3,1920]{2,0,1:T(1,128)S(1)}, f32[1,3,1920]{2,0,1:T(1,128)}, u32[]{:S(2)}) copy-start(f32[1,3,1920]{2,0,1:T(1,128)} %get-tuple-element.21) | copy-start | bytes 69124
  137.1 10.1 %all-to-all-start.3 = ((bf16[8,25,240]{2,1,0:T(8,128)(2,1)}), bf16[8,25,240]{2,1,0:T(8,128)(2,1)S(1)}, u32[]{:S(2)}, u32[]{:S(2)}) async-start(bf16[8,25,240]{2,1,0:T(8,128)(2,1)} %convolution_convert_fusion.5), calls=%async_computation.3 | async-start | bytes 262144 | tf_op jit(solution)/shard_map/all_to_all | solution.py:193
  147.3 27.7 %copy-start.6 = (f32[1,25,8,240]{3,2,0,1:T(8,128)}, f32[1,25,8,240]{3,2,0,1:T(8,128)S(1)}, u32[]{:S(2)}) copy-start(f32[1,25,8,240]{3,2,0,1:T(8,128)S(1)} %copy.178) | copy-start | bytes 576004
  147.6 7.7 %collective-permute-start = (bf16[1,25,1920]{2,1,0:T(8,128)(2,1)S(1)}, bf16[1,25,1920]{2,1,0:T(8,128)(2,1)S(1)}, u32[]{:S(2)}, u32[]{:S(2)}) collective-permute-start(bf16[1,25,1920]{2,1,0:T(8,128)(2,1)S(1)} %fusion.46), channel_id=1, source_target_pairs={{0,8},{8,16},{16,24},{1,9},{9,17},{17,25},{2,10},{10,18},{18,26},{... | collective-permute-start | bytes 288008 | tf_op jit(solution)/shard_map/ppermute | solution.py:15
  175.0 12.6 %copy-start.10 = (bf16[30,1920]{1,0:T(8,128)(2,1)S(1)}, bf16[30,1920]{1,0:T(8,128)(2,1)}, u32[]{:S(2)}) copy-start(bf16[30,1920]{1,0:T(8,128)(2,1)} %get-tuple-element.7) | copy-start | bytes 345604
  179.2 16.6 %all-to-all-start.4 = ((bf16[8,25,3,240]{3,1,2,0:T(8,128)(2,1)}), bf16[8,25,3,240]{3,1,2,0:T(8,128)(2,1)}, u32[]{:S(2)}, u32[]{:S(2)}) async-start(bf16[8,25,3,240]{3,1,2,0:T(8,128)(2,1)} %copy.187), calls=%async_computation.4 | async-start | bytes 786432 | tf_op jit(solution)/shard_map/all_to_all | solution.py:74
  199.2 9.7 %copy-start.2 = (bf16[1,25,3,1920]{3,1,2,0:T(8,128)(2,1)}, bf16[1,25,3,1920]{3,1,2,0:T(8,128)(2,1)S(1)}, u32[]{:S(2)}) copy-start(bf16[1,25,3,1920]{3,1,2,0:T(8,128)(2,1)S(1)} %all_to_all.72) | copy-start | bytes 864004
  209.5 7.1 %slice-start.1 = ((bf16[1,25,3,1920]{3,1,2,0:T(8,128)(2,1)}), bf16[1,25,1,1920]{3,1,2,0:T(8,128)(2,1)S(1)}, s32[]{:S(2)}) async-start(bf16[1,25,3,1920]{3,1,2,0:T(8,128)(2,1)} %copy-done.2), calls=%async_computation.8 | async-start | bytes 245760 | tf_op jit(solution)/shard_map/slice | solution.py:80
  215.5 0.8 copy-start.5
  217.6 12.0 %copy-start.7 = (f32[1,25,8,240]{3,2,0,1:T(8,128)S(1)}, f32[1,25,8,240]{3,2,0,1:T(8,128)}, u32[]{:S(2)}) copy-start(f32[1,25,8,240]{3,2,0,1:T(8,128)} %copy-done.6) | copy-start | bytes 576004
  225.3 29.4 %all-to-all-start.5 = ((bf16[8,1,25,1920]{3,2,1,0:T(8,128)(2,1)}), bf16[8,1,25,1920]{3,2,1,0:T(8,128)(2,1)}, u32[]{:S(2)}, u32[]{:S(2)}) async-start(bf16[8,1,25,1920]{3,2,1,0:T(8,128)(2,1)} %stack.12), calls=%async_computation.5 | async-start | bytes 1966080 | tf_op jit(solution)/shard_map/all_to_all | solution.py:109
  257.3 10.8 %all-to-all-start.6 = ((bf16[8,25,240]{2,1,0:T(8,128)(2,1)}), bf16[8,25,240]{2,1,0:T(8,128)(2,1)}, u32[]{:S(2)}, u32[]{:S(2)}) async-start(bf16[8,25,240]{2,1,0:T(8,128)(2,1)} %convolution_convert_fusion.4), calls=%async_computation.6 | async-start | bytes 262144 | tf_op jit(solution)/shard_map/all_to_all | solution.py:193
